TPU v7x, 32 devices: a whole 2x2x4 slice. The times are simulated.
32 devices in a mesh: coil: 4 (over x, core), slab: 8 (over z, y).
Axes of the slice: x: 2, y: 2, z: 4, core: 2. Of those that a mesh axis runs over, the one named last changes fastest.
Arguments:
- kspace_data: bfloat16 [32, 2, 128, 128, 128], P('coil', None, None, 'slab'), may hold values from -4 to 4
- coil_maps: bfloat16 [32, 2, 128, 128, 128], P('coil', None, 'slab'), may hold values from -1.796875 to 1.796875
- sample_mask: int32 [32, 128, 128], P('coil', None, 'slab'), may hold values 0 or 1
- initial_image: float32 [2, 128, 128, 128], P(None, 'slab', 'coil'), may hold values from -6 to 6
Outputs:
- image: float32 [2, 128, 128, 128], P(None, 'slab', 'coil')
All inputs are finite; a program needn't handle non-finite values. No bound on the sum of `sample_mask` on one device may be relied on, other than what follows from the above.
Results may differ from a plain program's by a relative error of at most 0.0045.
Values may be sent and summed in bfloat16 or wider, within the bound.
A program may use at most 128 MiB of HBM per device.

v0:
```python
import math

import jax
import jax.numpy as jnp
from jax import lax
from jax.sharding import PartitionSpec as P

NX = 128
NY = 128
NZ = 128
ITERS = 2


dual_step = 0.25
primal_step = 0.25
tv_weight = 0.5


def from_behind(block, axis, distance):
    devices = range(lax.axis_size(axis))
    route = [(i - distance, i) for i in devices if i - distance in devices]
    return lax.ppermute(block, axis, route)


def dft_table(length, inverse):
    counter = jnp.arange(length, dtype=jnp.int32)
    product = counter[:, None] * counter[None, :] % length
    phase = 2.0 * math.pi / length * product.astype(jnp.float32)
    scale = 1.0 / math.sqrt(length)
    real_part = jnp.cos(phase) * scale
    imag_part = jnp.sin(phase) * scale
    if not inverse:
        imag_part = -imag_part
    table = jnp.stack([jnp.stack([real_part, imag_part]), jnp.stack([-imag_part, real_part])])
    return table.astype(jnp.bfloat16)


def data_term(guess, coil_maps, kspace_data, sample_mask, dual_data, tables):
    forward_x, forward_y, forward_z, inverse_x, inverse_y, inverse_z = tables
    maps_real = coil_maps[:, 0].astype(jnp.float32)
    maps_imag = coil_maps[:, 1].astype(jnp.float32)
    pieces = jnp.stack(
        [maps_real * guess[0] - maps_imag * guess[1], maps_real * guess[1] + maps_imag * guess[0]],
        1,
    ).astype(jnp.bfloat16)
    pieces = jnp.einsum(
        "ckzyx,kjxw->cjzyw", pieces, forward_x, preferred_element_type=jnp.float32
    ).astype(jnp.bfloat16)
    pieces = jnp.einsum(
        "ckzyx,kjyv->cjzvx", pieces, forward_y, preferred_element_type=jnp.float32
    ).astype(jnp.bfloat16)
    spectrum = jnp.einsum(
        "ckzyx,kjzw->cjwyx",
        lax.all_to_all(pieces, "slab", split_axis=3, concat_axis=2, tiled=True),
        forward_z,
        preferred_element_type=jnp.float32,
    )
    sampled = sample_mask[:, None, :, :, None].astype(jnp.float32)
    dual_new = (
        dual_data + dual_step * (sampled * (spectrum - kspace_data.astype(jnp.float32)))
    ) / (1.0 + dual_step)
    back_field = jnp.einsum(
        "ckzyx,kjzw->cjwyx",
        dual_new.astype(jnp.bfloat16),
        inverse_z,
        preferred_element_type=jnp.float32,
    ).astype(jnp.bfloat16)
    back_field = jnp.einsum(
        "ckzyx,kjyv->cjzvx",
        lax.all_to_all(back_field, "slab", split_axis=2, concat_axis=3, tiled=True),
        inverse_y,
        preferred_element_type=jnp.float32,
    ).astype(jnp.bfloat16)
    back_field = jnp.einsum(
        "ckzyx,kjxw->cjzyw", back_field, inverse_x, preferred_element_type=jnp.float32
    )
    real_sum = jnp.sum(maps_real * back_field[:, 0] + maps_imag * back_field[:, 1], 0)
    imag_sum = jnp.sum(maps_real * back_field[:, 1] - maps_imag * back_field[:, 0], 0)
    return (jnp.stack([real_sum, imag_sum]), dual_new)


def tv_update(guess, duals):
    planes = guess.shape[1]
    plane_pos = lax.axis_index("slab") * planes + lax.broadcasted_iota(
        jnp.int32, (1, planes, 1, 1), 1
    )
    next_plane = from_behind(guess[:, :1], "slab", -1)
    ahead_z = jnp.concatenate([guess[:, 1:], next_plane], 1)
    grad_z = jnp.where(plane_pos < NZ - 1, ahead_z - guess, 0.0)
    grad_y = jnp.concatenate(
        [guess[:, :, 1:] - guess[:, :, :-1], jnp.zeros_like(guess[:, :, :1])], 2
    )
    grad_x = jnp.concatenate([guess[..., 1:] - guess[..., :-1], jnp.zeros_like(guess[..., :1])], 3)
    moved_z = duals[0] + dual_step * grad_z
    moved_y = duals[1] + dual_step * grad_y
    moved_x = duals[2] + dual_step * grad_x
    magnitude = jnp.sqrt(
        jnp.sum(moved_z * moved_z, 0)
        + jnp.sum(moved_y * moved_y, 0)
        + jnp.sum(moved_x * moved_x, 0)
    )
    factor = 1.0 / jnp.maximum(1.0, magnitude / tv_weight)
    dual_z = moved_z * factor
    dual_y = moved_y * factor
    dual_x = moved_x * factor
    prior_plane = from_behind(dual_z[:, -1:], "slab", 1)
    spread_z = jnp.concatenate([prior_plane, dual_z[:, :-1]], 1) - dual_z
    spread_y = jnp.concatenate([jnp.zeros_like(dual_y[:, :, :1]), dual_y[:, :, :-1]], 2) - dual_y
    spread_x = jnp.concatenate([jnp.zeros_like(dual_x[..., :1]), dual_x[..., :-1]], 3) - dual_x
    return ((dual_z, dual_y, dual_x), spread_z + spread_y + spread_x)


def on_device(kspace_data, coil_maps, sample_mask, initial_image):
    tables = (
        dft_table(NX, False),
        dft_table(NY, False),
        dft_table(NZ, False),
        dft_table(NX, True),
        dft_table(NY, True),
        dft_table(NZ, True),
    )
    dual_data = jnp.zeros(kspace_data.shape, jnp.float32)
    share_rows = initial_image.shape[2]
    current = initial_image
    guess = current
    duals = None
    for turn_index in range(ITERS):
        whole_guess = lax.all_gather(guess, "coil", axis=2, tiled=True)
        if duals is None:
            duals = (
                jnp.zeros_like(whole_guess),
                jnp.zeros_like(whole_guess),
                jnp.zeros_like(whole_guess),
            )
        data_grad, dual_data = data_term(
            whole_guess, coil_maps, kspace_data, sample_mask, dual_data, tables
        )
        data_grad = lax.psum_scatter(data_grad, "coil", scatter_dimension=2, tiled=True)
        duals, spread = tv_update(whole_guess, duals)
        spread_share = lax.dynamic_slice_in_dim(
            spread, lax.axis_index("coil") * share_rows, share_rows, 2
        )
        updated = current - primal_step * (data_grad + spread_share)
        guess = 2.0 * updated - current
        current = updated
    return current


def solution(mesh):
    placed = (
        P("coil", None, None, "slab", None),
        P("coil", None, "slab", None, None),
        P("coil", None, "slab"),
        P(None, "slab", "coil", None),
    )
    return jax.shard_map(
        on_device,
        mesh=mesh,
        in_specs=placed,
        out_specs=P(None, "slab", "coil", None),
        check_vma=False,
    )
```

profile of v0, /device:TPU:0, one launch (start us, length us, event | category | flops | bytes accessed | tf_op | source)
XLA Modules:
  0.0 1111.8 jit_solution(6184151116436738106)
XLA Ops:
  9.3 24.9 %all-gather.3.cloned.1.call-done = f32[2,16,128,128]{3,1,0,2:T(8,128)} async-done(((f32[2,16,32,128]{3,1,0,2:T(8,128)}), f32[2,16,128,128]{3,1,0,2:T(8,128)}) %all-gather.3.cloned.1.call-update) | async-done | bytes 2097168 | tf_op jit(solution)/shard_map/all_gather | solution.py:128
  43.0 9.0 fusion.8
  52.0 12.0 %copy.123 = bf16[8,2,16,128,128]{4,2,0,1,3:T(8,128)(2,1)} copy(bf16[8,2,16,128,128]{4,3,2,0,1:T(8,128)(2,1)} %fusion.8) | data formatting | bytes 16777216 | tf_op jit(solution)/shard_map/convert_element_type | solution.py:51
  69.9 183.3 %all-to-all-done = bf16[8,2,16,128,128]{4,2,0,1,3:T(8,128)(2,1)} async-done(((bf16[8,2,16,128,128]{4,2,0,1,3:T(8,128)(2,1)}), bf16[8,2,16,128,128]{4,2,0,1,3:T(8,128)(2,1)}, u32[]{:S(2)}, u32[]{:S(2)}) %all-to-all-start) | async-done | bytes 8388640 | tf_op jit(solution)/shard_map/all_to_all | solution.py:54
  253.2 9.1 copy.124
  262.3 12.3 %fusion.7 = (bf16[8,2,128,16,128]{4,2,3,0,1:T(8,128)(2,1)S(1)}, f32[2,128,8,16,128,1]{4,1,5,3,2,0:T(8,128)}) fusion(f32[8,128,16]{1,2,0:T(8,128)S(1)} %convert_element_type.129, bf16[8,2,128,16,128]{4,3,2,1,0:T(8,128)(2,1)} %param.4, bf16[8,2,128,16,128,1]{4,2,1,3,0,5:T(8,128)(2,1)} %bitcast.269, bf16[1,2,128,128]{2,3,0,1:T(8,128)(2,1)S(1)} %get-tuple-element.28, ...), kind=kOutput, calls=%fused_computation.33 | convolution fusion | flops 2168717312 | bytes 42139648 | tf_op jit(solution)/shard_map/ckzyx,kjzw->cjwyx/dot_general | solution.py:52
  279.1 12.0 %copy.128 = bf16[8,2,128,16,128]{4,3,0,1,2:T(8,128)(2,1)} copy(bf16[8,2,128,16,128]{4,2,3,0,1:T(8,128)(2,1)} %fusion.9) | data formatting | bytes 16777216 | tf_op jit(solution)/shard_map/convert_element_type | solution.py:67
  291.1 189.0 %all_to_all.72 = bf16[8,2,128,16,128]{4,3,0,1,2:T(8,128)(2,1)} all-to-all(bf16[8,2,128,16,128]{4,3,0,1,2:T(8,128)(2,1)} %copy.128), channel_id=1, replica_groups=mesh['coil'=4,'slab'=8] {'slab'}, dimensions={2} | all-to-all | bytes 16777216 | tf_op jit(solution)/shard_map/all_to_all | solution.py:70
  480.2 9.1 copy.130
  489.3 10.3 convolution_bitcast_fusion.1
  499.5 10.0 fusion.17
  535.5 8.4 reduce-scatter.3.cloned.1.call-done
  547.2 22.7 %all-gather.5.cloned.1.call-done = f32[2,16,128,128]{3,1,0,2:T(8,128)} async-done(((f32[2,16,32,128]{3,1,0,2:T(8,128)}), f32[2,16,128,128]{3,1,0,2:T(8,128)}) %all-gather.5.cloned.1.call-update) | async-done | bytes 2097168 | tf_op jit(solution)/shard_map/all_gather | solution.py:128
  580.5 9.0 fusion.10
  589.5 12.0 %copy.143 = bf16[8,2,16,128,128]{4,2,0,1,3:T(8,128)(2,1)} copy(bf16[8,2,16,128,128]{4,3,2,0,1:T(8,128)(2,1)} %fusion.10) | data formatting | bytes 16777216 | tf_op jit(solution)/shard_map/convert_element_type | solution.py:51
  601.5 189.6 %all_to_all.73 = bf16[8,2,16,128,128]{4,2,0,1,3:T(8,128)(2,1)} all-to-all(bf16[8,2,16,128,128]{4,2,0,1,3:T(8,128)(2,1)} %copy.143), channel_id=1, replica_groups=mesh['coil'=4,'slab'=8] {'slab'}, dimensions={3} | all-to-all | bytes 16777216 | tf_op jit(solution)/shard_map/all_to_all | solution.py:54
  791.0 16.3 %copy.145 = bf16[8,2,8,16,16,128]{5,4,3,2,1,0:T(8,128)(2,1)} copy(bf16[8,2,8,16,16,128]{5,3,0,1,4,2:T(8,128)(2,1)} %bitcast.273) | data formatting | bytes 16777216 | tf_op jit(solution)/shard_map/all_to_all | solution.py:54
  807.3 21.2 %fusion.6 = bf16[8,2,128,16,128]{4,2,3,0,1:T(8,128)(2,1)} fusion(f32[2,128,8,16,128,1]{4,1,5,3,2,0:T(8,128)} %get-tuple-element.34, f32[8,128,16]{1,2,0:T(8,128)S(1)} %convert_element_type.129, bf16[8,2,128,16,128]{4,3,2,1,0:T(8,128)(2,1)} %param.4, bf16[8,2,128,16,128]{4,3,2,1,0:T(8,128)(2,1)} %bitcast.278, ...), kind=kOutput, calls=%fused_computation.24 | convolution fusion | flops 2189688832 | bytes 42139648 | tf_op jit(solution)/shard_map/ckzyx,kjzw->cjwyx/dot_general | solution.py:52
  836.5 12.0 %copy.149 = bf16[8,2,128,16,128]{4,3,0,1,2:T(8,128)(2,1)} copy(bf16[8,2,128,16,128]{4,2,3,0,1:T(8,128)(2,1)} %fusion.11) | data formatting | bytes 16777216 | tf_op jit(solution)/shard_map/convert_element_type | solution.py:67
  848.5 188.8 %all_to_all.74 = bf16[8,2,128,16,128]{4,3,0,1,2:T(8,128)(2,1)} all-to-all(bf16[8,2,128,16,128]{4,3,0,1,2:T(8,128)(2,1)} %copy.149), channel_id=1, replica_groups=mesh['coil'=4,'slab'=8] {'slab'}, dimensions={2} | all-to-all | bytes 16777216 | tf_op jit(solution)/shard_map/all_to_all | solution.py:70
  1037.3 9.1 copy.151
  1046.4 10.3 convolution_bitcast_fusion
  1056.7 10.0 fusion.25
  1090.6 10.9 reduce-scatter.5.cloned.1.call-done
  (89 shorter events, 96.5 us)
Async XLA Ops:
  6.5 27.7 %all-gather.3.cloned.1.call-start = ((), (), s32[]{:S(2)}) async-start(), calls=%async_computation.6 | async-start | bytes 2621440 | tf_op jit(solution)/shard_map/all_gather | solution.py:128
  34.2 4.0 copy-start.1
  64.0 5.9 copy-start.11
  64.0 189.2 %all-to-all-start = ((bf16[8,2,16,128,128]{4,2,0,1,3:T(8,128)(2,1)}), bf16[8,2,16,128,128]{4,2,0,1,3:T(8,128)(2,1)}, u32[]{:S(2)}, u32[]{:S(2)}) async-start(bf16[8,2,16,128,128]{4,2,0,1,3:T(8,128)(2,1)} %copy.123), calls=%async_computation | async-start | bytes 16777216 | tf_op jit(solution)/shard_map/all_to_all | solution.py:54
  69.6 474.3 %reduce-scatter.3.cloned.1.call-start = ((), (), s32[]{:S(2)}) async-start(), calls=%async_computation.7 | async-start | bytes 2621440 | tf_op jit(solution)/shard_map/reduce_scatter | solution.py:138
  511.6 3.4 copy-start
  515.0 54.9 %all-gather.5.cloned.1.call-start = ((), (), s32[]{:S(2)}) async-start(), calls=%async_computation.8 | async-start | bytes 2621440 | tf_op jit(solution)/shard_map/all_gather | solution.py:128
  515.2 6.9 collective-permute-start
  526.5 1.3 copy-start.6
  526.5 17.4 %copy-start.3 = (f32[2,16,128,128]{3,1,0,2:T(8,128)S(1)}, f32[2,16,128,128]{3,1,0,2:T(8,128)}, u32[]{:S(2)}) copy-start(f32[2,16,128,128]{3,1,0,2:T(8,128)} %get-tuple-element.26) | copy-start | bytes 6291460
  526.5 17.4 %copy-start.10 = (f32[2,16,32,128]{3,2,1,0:T(8,128)S(1)}, f32[2,16,32,128]{3,2,1,0:T(8,128)}, u32[]{:S(2)}) copy-start(f32[2,16,32,128]{3,2,1,0:T(8,128)} %param.7) | copy-start | bytes 1572868
  528.0 7.5 collective-permute-start.1
  547.2 554.4 %reduce-scatter.5.cloned.1.call-start = ((), (), s32[]{:S(2)}) async-start(), calls=%async_computation.9 | async-start | bytes 2621440 | tf_op jit(solution)/shard_map/reduce_scatter | solution.py:138
  1068.8 3.3 copy-start.2
  1072.3 6.9 collective-permute-start.2
  1074.1 1.6 copy-start.4
  1076.3 1.8 copy-start.5
  1076.3 2.8 copy-start.7
  1083.3 4.9 copy-start.8
  1083.3 18.3 %copy-start.9 = (f32[2,16,32,128]{3,1,0,2:T(8,128)S(1)}, f32[2,16,32,128]{3,1,0,2:T(8,128)}, u32[]{:S(2)}) copy-start(f32[2,16,32,128]{3,1,0,2:T(8,128)} %get-tuple-element.12) | copy-start | bytes 1572868
  1083.4 7.2 collective-permute-start.3
Sparse Core Ops, SparseCore 0:
  8.9 25.2 all-gather.2
  515.1 28.8 reduce-scatter.2
  547.3 22.5 all-gather.4
  1072.3 29.2 reduce-scatter.4
where the time goes:
time: 1120 us; the launch traced here: 1110 us
  blocking collectives  567 us (51%)
  waiting for transfers between devices  255 us (23%)
  local copies, waits for them, and re-layouts  119 us (11%)
  matrix products  84.5 us (8%)
  other arithmetic  53.8 us (5%)
  starting transfers between devices  18 us (2%)
  between operations  14 us (1%)
    all_to_all x2, blocking collectives, data_term(): lax.all_to_all(back_field, 'slab', split_axis=2, concat_axis=3, tiled=True)  378 us
    all_to_all x1, blocking collectives, data_term(): lax.all_to_all(pieces, 'slab', split_axis=3, concat_axis=2, tiled=True)  190 us
    all_to_all x1, waiting for transfers between devices, data_term(): lax.all_to_all(pieces, 'slab', split_axis=3, concat_axis=2, tiled=True)  183 us
    all_gather x2, waiting for transfers between devices, on_device(): whole_guess = lax.all_gather(guess, 'coil', axis=2, tiled=True)  47.6 us
    dot_general x2, matrix products, data_term(): jnp.einsum('ckzyx,kjzw->cjwyx', lax.all_to_all(pieces, 'slab', split_axis...  33.5 us
    all_to_all x2, local copies, waits for them, and re-layouts, data_term(): lax.all_to_all(pieces, 'slab', split_axis=3, concat_axis=2, tiled=True)  25.4 us
    convert_element_type x2, local copies, waits for them, and re-layouts, data_term(): back_field = jnp.einsum('ckzyx,kjzw->cjwyx', dual_new.astype(jnp.bfloat16...  24 us
    convert_element_type x2, local copies, waits for them, and re-layouts, data_term(): pieces = jnp.einsum('ckzyx,kjyv->cjzvx', pieces, forward_y, preferred_ele...  24 us
  transfers between devices with their start and end apart: 9, of which 8 were waited for; matrix products, arithmetic and copies ran while one was open for 2% of the time, Pallas kernels for 0%

commit v1 on v0

v1 whole, which is shorter than its diff:
```python
import functools
import math

import jax
import jax.numpy as jnp
import ml_dtypes
import numpy as np
from jax import lax
from jax.experimental import pallas as pl
from jax.experimental.pallas import tpu as pltpu
from jax.sharding import PartitionSpec as P

ITERS = 2

dual_step = 0.25
primal_step = 0.25
tv_weight = 0.5
f32 = jnp.float32
bf16 = jnp.bfloat16


def from_behind(block, axis, distance):
    devices = range(lax.axis_size(axis))
    route = [(i - distance, i) for i in devices if i - distance in devices]
    return lax.ppermute(block, axis, route)


def dft_table(length, inverse):
    counter = np.arange(length)
    phase = 2.0 * math.pi / length * (np.outer(counter, counter) % length)
    real_part = np.cos(phase) / math.sqrt(length)
    imag_part = np.sin(phase) / math.sqrt(length)
    if not inverse:
        imag_part = -imag_part
    table = np.stack([np.stack([real_part, imag_part]), np.stack([-imag_part, real_part])])
    return table.astype(ml_dtypes.bfloat16)


def on_right(table):
    n = table.shape[2]
    return jnp.asarray(table.transpose(0, 2, 1, 3).reshape(2 * n, 2 * n))


def on_left(table):
    n = table.shape[2]
    return jnp.asarray(table.transpose(1, 3, 0, 2).reshape(2 * n, 2 * n))


def plane(ref, coil, part):
    block = ref[:, coil, 0, part]
    return block.reshape(block.shape[0] * block.shape[1], block.shape[2])


def dot(a, b, dims=((1,), (0,))):
    return lax.dot_general(a, b, (dims, ((), ())), preferred_element_type=f32)


def combine(out_ref, maps_ref, images, group):
    nz, ny = out_ref.shape[2:]
    real_sum = imag_sum = None
    for coil in range(group):
        real = images[coil * nz : (coil + 1) * nz, :ny]
        imag = images[coil * nz : (coil + 1) * nz, ny:]
        maps_real = plane(maps_ref, coil, 0).astype(f32)
        maps_imag = plane(maps_ref, coil, 1).astype(f32)
        real_term = maps_real * real + maps_imag * imag
        imag_term = maps_real * imag - maps_imag * real
        real_sum = real_term if coil == 0 else real_sum + real_term
        imag_sum = imag_term if coil == 0 else imag_sum + imag_term

    @pl.when(pl.program_id(1) == 0)
    def _():
        out_ref[0, 0] = real_sum
        out_ref[0, 1] = imag_sum

    @pl.when(pl.program_id(1) > 0)
    def _():
        out_ref[0, 0] += real_sum
        out_ref[0, 1] += imag_sum


def normal_kernel(group, guess_ref, maps_ref, mask_ref, fy_ref, fz_ref, gz_ref, gy_ref, out_ref):
    nz, ny = out_ref.shape[2:]
    guess_real = guess_ref[0, 0]
    guess_imag = guess_ref[0, 1]
    rows = []
    for coil in range(group):
        maps_real = plane(maps_ref, coil, 0).astype(f32)
        maps_imag = plane(maps_ref, coil, 1).astype(f32)
        real = maps_real * guess_real - maps_imag * guess_imag
        imag = maps_real * guess_imag + maps_imag * guess_real
        rows.append(jnp.concatenate([real.astype(bf16), imag.astype(bf16)], 1))
    pieces = dot(jnp.concatenate(rows, 0), fy_ref[...]).astype(bf16)
    pieces = jnp.concatenate(
        [
            jnp.concatenate(
                [pieces[c * nz : (c + 1) * nz, j * ny : (j + 1) * ny] for c in range(group)], 1
            )
            for j in range(2)
        ],
        0,
    )
    spectrum = dot(fz_ref[...], pieces).astype(bf16)
    mask = jnp.concatenate([mask_ref[c] for c in range(group)], 1)
    spectrum = spectrum * jnp.concatenate([mask, mask], 0)
    pieces = dot(gz_ref[...], spectrum).astype(bf16)
    pieces = jnp.concatenate(
        [
            jnp.concatenate(
                [pieces[j * nz : (j + 1) * nz, c * ny : (c + 1) * ny] for j in range(2)], 1
            )
            for c in range(group)
        ],
        0,
    )
    combine(out_ref, maps_ref, dot(pieces, gy_ref[...]), group)


def data_kernel(group, data_ref, maps_ref, gy_ref, out_ref):
    columns = jnp.concatenate(
        [
            jnp.concatenate([plane(data_ref, c, 0), plane(data_ref, c, 1)], 0)
            for c in range(group)
        ],
        1,
    )
    combine(out_ref, maps_ref, dot(columns, gy_ref[...], ((0,), (0,))), group)


def whole(shape):
    return pl.BlockSpec(shape, lambda x, c: (0,) * len(shape))


def coil_blocks(array, group):
    src, _, _, parts, planes, cols = array.shape
    return pl.BlockSpec((src, group, 1, parts, planes, cols), lambda x, c: (0, c, x, 0, 0, 0))


def call(kernel, group, operands, specs, shape, coils, flops, nbytes):
    return pl.pallas_call(
        functools.partial(kernel, group),
        out_shape=jax.ShapeDtypeStruct(shape, f32),
        grid=(shape[0], coils // group),
        in_specs=specs,
        out_specs=pl.BlockSpec((1,) + shape[1:], lambda x, c: (x, 0, 0, 0)),
        compiler_params=pltpu.CompilerParams(
            dimension_semantics=("arbitrary", "arbitrary"), vmem_limit_bytes=48 * 2**20
        ),
        cost_estimate=pl.CostEstimate(flops=flops, bytes_accessed=nbytes, transcendentals=0),
    )(*operands)


def coil_group(coils):
    return max(g for g in (1, 2, 4) if coils % g == 0)


def apply_normal(guess, maps, mask, tables):
    coils = maps.shape[1]
    group = coil_group(coils)
    shape = guess.shape
    specs = [
        pl.BlockSpec((1,) + shape[1:], lambda x, c: (x, 0, 0, 0)),
        coil_blocks(maps, group),
        pl.BlockSpec((group,) + mask.shape[1:], lambda x, c: (c, 0, 0)),
    ] + [whole(t.shape) for t in tables]
    cells = coils * shape[0] * shape[2] * shape[3]
    return call(
        normal_kernel, group, (guess, maps, mask) + tables, specs, shape, coils, cells * 4096, cells * 4
    )


def apply_data(data, maps, table, shape):
    coils = maps.shape[1]
    group = coil_group(coils)
    specs = [coil_blocks(data, group), coil_blocks(maps, group), whole(table.shape)]
    cells = coils * shape[0] * shape[2] * shape[3]
    return call(data_kernel, group, (data, maps, table), specs, shape, coils, cells * 1024, cells * 8)


def exchange(blocks):
    got = lax.all_to_all(blocks, "slab", split_axis=0, concat_axis=0, tiled=True)
    if got.shape[4] % 16:
        src, coils, width, parts, share, cols = got.shape
        got = got.transpose(1, 2, 3, 0, 4, 5).reshape(1, coils, width, parts, src * share, cols)
    return got


def tv_update(guess, duals):
    width = guess.shape[0]
    size = lax.axis_size("slab") * width
    pos = lax.axis_index("slab") * width + lax.broadcasted_iota(jnp.int32, (width, 1, 1, 1), 0)
    ahead_x = jnp.concatenate([guess[1:], from_behind(guess[:1], "slab", -1)], 0)
    grad_x = jnp.where(pos < size - 1, ahead_x - guess, 0.0)
    grad_z = jnp.concatenate(
        [guess[:, :, 1:] - guess[:, :, :-1], jnp.zeros_like(guess[:, :, :1])], 2
    )
    grad_y = jnp.concatenate([guess[..., 1:] - guess[..., :-1], jnp.zeros_like(guess[..., :1])], 3)
    moved = [dual_step * grad for grad in (grad_z, grad_y, grad_x)]
    if duals is not None:
        moved = [dual + step for dual, step in zip(duals, moved)]
    magnitude = jnp.sqrt(sum(jnp.sum(w * w, 1, keepdims=True) for w in moved))
    factor = 1.0 / jnp.maximum(1.0, magnitude / tv_weight)
    dual_z, dual_y, dual_x = [w * factor for w in moved]
    prior = from_behind(dual_x[-1:], "slab", 1)
    spread_x = jnp.concatenate([prior, dual_x[:-1]], 0) - dual_x
    spread_z = jnp.concatenate([jnp.zeros_like(dual_z[:, :, :1]), dual_z[:, :, :-1]], 2) - dual_z
    spread_y = jnp.concatenate([jnp.zeros_like(dual_y[..., :1]), dual_y[..., :-1]], 3) - dual_y
    return (dual_z, dual_y, dual_x), spread_z + spread_y + spread_x


def on_device(kspace_data, coil_maps, sample_mask, initial_image):
    slabs = lax.axis_size("slab")
    groups = lax.axis_size("coil")
    coils, _, planes, ny, nx = coil_maps.shape
    nz = kspace_data.shape[2]
    shares = kspace_data.shape[3]
    rows = initial_image.shape[2]
    width = nx // slabs
    forward_y, inverse_y = dft_table(ny, False), dft_table(ny, True)
    forward_z, inverse_z = dft_table(nz, False), dft_table(nz, True)
    inverse_x = jnp.asarray(dft_table(nx, True))
    tables = (on_right(forward_y), on_left(forward_z), on_left(inverse_z), on_right(inverse_y))

    image = initial_image.reshape(2, planes, rows, slabs, width).transpose(3, 4, 0, 2, 1)
    image = lax.all_to_all(
        image.reshape(slabs, -1), "slab", split_axis=0, concat_axis=0, tiled=True
    ).reshape(slabs, width, 2, rows, planes)
    image = image.transpose(1, 2, 3, 0, 4).reshape(width, 2, rows, nz)
    image = lax.all_gather(image, "coil", axis=2, tiled=True).swapaxes(2, 3)
    mask = lax.all_gather(sample_mask.astype(bf16), "slab", axis=2, tiled=True)

    maps = coil_maps.reshape(coils, 2, planes, ny, slabs, width).transpose(4, 0, 5, 1, 2, 3)
    maps, image, mask = lax.optimization_barrier((maps, image, mask))
    maps = exchange(maps)

    data = kspace_data * sample_mask[:, None, :, :, None].astype(bf16)
    data = jnp.einsum("ckzyx,kjxw->cjzyw", data, inverse_x, preferred_element_type=f32).astype(bf16)
    data = jnp.einsum(
        "ckzyx,kjzw->cjywx", data, jnp.asarray(inverse_z), preferred_element_type=f32
    ).astype(bf16)
    data = data.reshape(coils, 2, shares, nz, slabs, width).transpose(4, 0, 5, 1, 2, 3)
    data, maps = lax.optimization_barrier((data, maps))
    data = exchange(data)

    normal = apply_normal(image, maps, mask, tables)
    duals, spread = tv_update(image, None)
    data, normal, duals, spread = lax.optimization_barrier((data, normal, duals, spread))
    back_data = apply_data(data, maps, tables[3], image.shape)
    scale = dual_step / (1.0 + dual_step)
    data_grad = lax.psum(scale * (normal - back_data), "coil")
    updated = image - primal_step * (data_grad + spread)
    guess = 2.0 * updated - image
    normal = apply_normal(guess, maps, mask, tables)
    _, spread = tv_update(guess, duals)
    known = updated - primal_step * (data_grad / (1.0 + dual_step) + spread)
    share = known / groups - (primal_step * scale) * (normal - back_data)
    share = lax.psum_scatter(share.swapaxes(2, 3), "coil", scatter_dimension=2, tiled=True)
    share = share.reshape(width, 2, rows, slabs, planes).transpose(3, 1, 4, 2, 0)
    share = lax.all_to_all(
        share.reshape(slabs, -1), "slab", split_axis=0, concat_axis=0, tiled=True
    ).reshape(slabs, 2, planes, rows, width)
    return share.transpose(1, 2, 3, 0, 4).reshape(2, planes, rows, nx)


def solution(mesh):
    placed = (
        P("coil", None, None, "slab", None),
        P("coil", None, "slab", None, None),
        P("coil", None, "slab"),
        P(None, "slab", "coil", None),
    )
    return jax.shard_map(
        on_device,
        mesh=mesh,
        in_specs=placed,
        out_specs=P(None, "slab", "coil", None),
        check_vma=False,
    )
```

time: 1120 us -> 749 us (0.67)
  blocking collectives: 567 us -> 72.5 us
  waiting for transfers between devices: 255 us -> 364 us
  Pallas kernels: 0 us -> 83.2 us
  matrix products: 84.5 us -> 9.21 us
  starting transfers between devices: 18 us -> 66.4 us
  local copies, waits for them, and re-layouts: 119 us -> 91 us
  other arithmetic: 53.8 us -> 41.3 us
    all_to_all x3 -> x2, blocking collectives: 567 us -> 41.6 us  [the longest x1 21.6 us: on_device(): lax.all_to_all(image.reshape(slabs, -1), 'slab', split_axis=0, concat_axi...]
    psum x0 -> x1, waiting for transfers between devices: none -> 100 us  [on_device(): data_grad = lax.psum(scale * (normal - back_data), 'coil')]
    pallas_call x0 -> x3, Pallas kernels: none -> 83.2 us  [call(): pl.pallas_call(functools.partial(kernel, group), out_shape=jax.ShapeDtype...]
    dot_general x8 -> x1, matrix products: 84.5 us -> 9.21 us  [on_device(): jnp.einsum('ckzyx,kjzw->cjywx', data, jnp.asarray(inverse_z), preferred_e...]
    convert_element_type x4 -> x1, local copies, waits for them, and re-layouts: 48 us -> 0.18 us  [on_device(): mask = lax.all_gather(sample_mask.astype(bf16), 'slab', axis=2, tiled=True)]
    all_gather x2 -> x1, waiting for transfers between devices: 47.6 us -> 0.01 us  [on_device(): image = lax.all_gather(image, 'coil', axis=2, tiled=True).swapaxes(2, 3)]
    ppermute x4, waiting for transfers between devices: 5.13 us -> 51.9 us  [from_behind(): return lax.ppermute(block, axis, route)]
    ppermute x4, starting transfers between devices: 12 us -> 56.1 us  [from_behind(): return lax.ppermute(block, axis, route)]
  transfers between devices with their start and end apart: 9 -> 9, of which waited for: 8 -> 7; matrix products, arithmetic and copies ran while one was open for 2% -> 10% of each run, Pallas kernels for 0% -> 8%
where the time goes in v1:
time: 749 us; the launch traced here: 741 us
  waiting for transfers between devices  364 us (49%)
  local copies, waits for them, and re-layouts  91 us (12%)
  Pallas kernels  83.2 us (11%)
  blocking collectives  72.5 us (10%)
  starting transfers between devices  66.4 us (9%)
  other arithmetic  41.3 us (6%)
  between operations  14 us (2%)
  matrix products  9.21 us (1%)
    all_to_all x2, waiting for transfers between devices, exchange(): lax.all_to_all(blocks, 'slab', split_axis=0, concat_axis=0, tiled=True)  182 us
    psum x1, waiting for transfers between devices, on_device(): data_grad = lax.psum(scale * (normal - back_data), 'coil')  100 us
    pallas_call x3, Pallas kernels, call(): pl.pallas_call(functools.partial(kernel, group), out_shape=jax.ShapeDtype...  83.2 us
    ppermute x4, starting transfers between devices, from_behind(): return lax.ppermute(block, axis, route)  56.1 us
    ppermute x4, waiting for transfers between devices, from_behind(): return lax.ppermute(block, axis, route)  51.9 us
    all_gather x1, blocking collectives, on_device(): mask = lax.all_gather(sample_mask.astype(bf16), 'slab', axis=2, tiled=True)  30.9 us
    reduce_scatter x1, waiting for transfers between devices, on_device(): lax.psum_scatter(share.swapaxes(2, 3), 'coil', scatter_dimension=2, tiled...  29.7 us
    all_to_all x1, blocking collectives, on_device(): lax.all_to_all(image.reshape(slabs, -1), 'slab', split_axis=0, concat_axi...  21.6 us
  transfers between devices with their start and end apart: 9, of which 7 were waited for; matrix products, arithmetic and copies ran while one was open for 10% of the time, Pallas kernels for 8%

profile of v1, /device:TPU:0, one launch (start us, length us, event | category | flops | bytes accessed | tf_op | source)
XLA Modules:
  0.0 741.3 jit_solution(9962698347322002469)
XLA Ops:
  6.5 5.3 copy.69
  15.5 21.6 %all_to_all.30 = f32[8,1,16384]{2,1,0:T(1,128)S(1)} all-to-all(f32[8,1,16384]{2,1,0:T(1,128)S(1)} %all_to_all.24), channel_id=1, replica_groups=mesh['coil'=4,'slab'=8] {'slab'}, dimensions={0} | all-to-all | bytes 1048576 | tf_op jit(solution)/shard_map/all_to_all | solution.py:225
  46.0 12.0 %copy.42 = bf16[8,2,16,128,128]{3,4,2,1,0:T(8,128)(2,1)} copy(bf16[8,2,16,128,128]{4,3,2,1,0:T(8,128)(2,1)} %param.11) | data formatting | bytes 16777216 | tf_op args[1]
  58.1 16.4 %copy.86 = bf16[8,2,16,128,8,16]{3,2,1,5,0,4:T(8,128)(2,1)} copy(bf16[8,2,16,128,8,16]{3,5,4,2,1,0:T(8,128)(2,1)} %bitcast.68) | data formatting | bytes 16777216 | tf_op jit(solution)/shard_map/reshape | solution.py:232
  74.5 30.9 %all_gather.7 = bf16[8,128,128]{1,0,2:T(8,128)(2,1)S(1)} all-gather(bf16[8,128,16]{1,0,2:T(8,128)(2,1)S(1)} %copy_convert_fusion), channel_id=1, replica_groups=mesh['coil'=4,'slab'=8] {'slab'}, dimensions={2}, use_global_device_ids=true | all-gather | bytes 294912 | tf_op jit(solution)/shard_map/all_gather | solution.py:230
  107.4 5.1 all-to-all-start.1
  112.7 7.9 %multiply_bitcast_fusion = bf16[8,2,128,16,128,1]{4,3,2,1,0,5:T(8,128)(2,1)} fusion(bf16[8,2,128,16,128]{4,3,2,1,0:T(8,128)(2,1)} %param.10, bf16[8,128,16]{2,1,0:T(8,128)(2,1)S(1)} %copy.51), kind=kLoop, calls=%fused_computation.6 | loop fusion | flops 4194304 | bytes 16809984 | tf_op jit(solution)/shard_map/mul | solution.py:236
  120.6 9.2 %bitcast_convert_fusion = bf16[8,16,128,2,128]{4,2,3,1,0:T(8,128)(2,1)} fusion(bf16[2,2,128,128,1,1]{3,2,0,1,5,4:T(8,128)(2,1)S(1)} %copy-done.16, bf16[8,2,128,16,128,1]{4,3,2,1,0,5:T(8,128)(2,1)} %multiply_bitcast_fusion), kind=kOutput, calls=%fused_computation | convolution fusion | flops 4303355904 | bytes 16908288 | tf_op jit(solution)/shard_map/ckzyx,kjzw->cjywx/dot_general | solution.py:238
  129.8 16.3 %copy.85 = bf16[8,2,16,128,8,16]{3,2,1,5,0,4:T(8,128)(2,1)} copy(bf16[8,2,16,128,8,16]{3,5,4,1,2,0:T(8,128)(2,1)} %bitcast.77) | data formatting | bytes 16777216 | tf_op jit(solution)/shard_map/reshape | solution.py:241
  146.2 142.6 %all-to-all-done.1.maps_ref = bf16[8,8,16,2,16,128]{5,4,3,2,1,0:T(8,128)(2,1)} async-done(((bf16[8,8,16,2,16,128]{5,4,3,2,1,0:T(8,128)(2,1)}), bf16[8,8,16,2,16,128]{5,4,3,2,1,0:T(8,128)(2,1)}, u32[]{:S(2)}, u32[]{:S(2)}) %all-to-all-start.1) | async-done | bytes 8388640 | tf_op jit(solution)/shard_map/all_to_all | solution.py:181
  288.8 5.0 all-to-all-start.2
  297.0 47.5 %collective-permute-done = f32[1,2,128,128]{3,2,1,0:T(8,128)S(1)} collective-permute-done((f32[1,2,128,128]{3,2,1,0:T(8,128)S(1)}, f32[1,2,128,128]{3,2,1,0:T(8,128)S(1)}, u32[]{:S(2)}, u32[]{:S(2)}) %collective-permute-start) | collective-permute-done | bytes 131104 | tf_op jit(solution)/shard_map/ppermute | solution.py:25
  350.1 48.5 %collective-permute-start.1 = (f32[1,2,128,128]{3,2,1,0:T(8,128)S(1)}, f32[1,2,128,128]{3,2,1,0:T(8,128)S(1)}, u32[]{:S(2)}, u32[]{:S(2)}) collective-permute-start(f32[1,2,128,128]{3,2,1,0:T(8,128)S(1)} %slice.82), channel_id=1, source_target_pairs={{0,1},{1,2},{2,3},{3,4},{4,5},{5,6},{6,7},{8,9},{9,10},{10,11},{11... | collective-permute-start | bytes 393224 | tf_op jit(solution)/shard_map/ppermute | solution.py:25
  401.1 5.5 fusion.3
  406.6 30.3 %shard_map.100 = f32[16,2,128,128]{3,2,1,0:T(8,128)S(1)} custom-call(f32[16,2,128,128]{3,2,1,0:T(8,128)S(1)} %bitcast.61, bf16[8,8,16,2,16,128]{5,4,3,2,1,0:T(8,128)(2,1)} %all-to-all-done.1.maps_ref, bf16[8,128,128]{2,1,0:T(8,128)(2,1)S(1)} %copy.56.mask_ref, bf16[256,256]{1,0:T(8,128)(2,1)S(1)} %copy-done.7, bf16[256,256]{1,0:T(8,128)(2,1)S(1)} %copy-done.6, ...), custom_call_target="tpu_custom_call" | custom-call | flops 8589934592 | bytes 8388608 | tf_op jit(solution)/shard_map/pallas_call | solution.py:140
  438.2 38.9 %all-to-all-done.2.data_ref = bf16[8,8,16,2,16,128]{5,4,3,2,1,0:T(8,128)(2,1)} async-done(((bf16[8,8,16,2,16,128]{5,4,3,2,1,0:T(8,128)(2,1)}), bf16[8,8,16,2,16,128]{5,4,3,2,1,0:T(8,128)(2,1)}, u32[]{:S(2)}, u32[]{:S(2)}) %all-to-all-start.2) | async-done | bytes 8388640 | tf_op jit(solution)/shard_map/all_to_all | solution.py:181
  477.1 22.5 %shard_map.101 = f32[16,2,128,128]{3,2,1,0:T(8,128)S(1)} custom-call(bf16[8,8,16,2,16,128]{5,4,3,2,1,0:T(8,128)(2,1)} %all-to-all-done.2.data_ref, bf16[8,8,16,2,16,128]{5,4,3,2,1,0:T(8,128)(2,1)} %all-to-all-done.1.maps_ref, bf16[256,256]{1,0:T(8,128)(2,1)S(1)} %copy-done.6), custom_call_target="tpu_custom_call" | custom-call | flops 2147483648 | bytes 16777216 | tf_op jit(solution)/shard_map/pallas_call | solution.py:140
  502.8 100.5 %all-reduce.10.cloned.1.call-done = f32[16,2,128,128]{3,2,1,0:T(8,128)} async-done(((f32[16,2,128,128]{3,2,1,0:T(8,128)}), f32[16,2,128,128]{3,2,1,0:T(8,128)}) %all-reduce.10.cloned.1.call-update) | async-done | bytes 2097168 | tf_op jit(solution)/shard_map/psum | solution.py:250
  618.7 4.3 broadcast_multiply_fusion.2
  623.0 4.3 collective-permute-start.3
  627.3 30.4 %shard_map.102 = f32[16,2,128,128]{3,2,1,0:T(8,128)S(1)} custom-call(f32[16,2,128,128]{3,2,1,0:T(8,128)S(1)} %copy-done.1, bf16[8,8,16,2,16,128]{5,4,3,2,1,0:T(8,128)(2,1)} %all-to-all-done.1.maps_ref, bf16[8,128,128]{2,1,0:T(8,128)(2,1)S(1)} %copy.56.mask_ref, bf16[256,256]{1,0:T(8,128)(2,1)S(1)} %copy-done.7, bf16[256,256]{1,0:T(8,128)(2,1)S(1)} %copy-done.6, ...), custom_call_target="tpu_custom_call" | custom-call | flops 8589934592 | bytes 8388608 | tf_op jit(solution)/shard_map/pallas_call | solution.py:140
  659.4 5.2 fusion.13
  667.7 29.7 %reduce-scatter.2.cloned.1.call-done = f32[16,2,32,128]{3,0,1,2:T(8,128)} async-done(((f32[16,2,128,128]{3,0,1,2:T(8,128)}), f32[16,2,32,128]{3,0,1,2:T(8,128)}) %reduce-scatter.2.cloned.1.call-update) | async-done | bytes 524304 | tf_op jit(solution)/shard_map/reduce_scatter | solution.py:257
  705.5 20.0 %all_to_all.31 = f32[8,1,16384]{2,1,0:T(1,128)S(1)} all-to-all(f32[8,1,16384]{2,1,0:T(1,128)S(1)} %all_to_all.25), channel_id=1, replica_groups=mesh['coil'=4,'slab'=8] {'slab'}, dimensions={0} | all-to-all | bytes 1048576 | tf_op jit(solution)/shard_map/all_to_all | solution.py:259
  (87 shorter events, 67.3 us)
Async XLA Ops:
  6.5 98.8 %all-gather.2.cloned.1.call-start = ((), (), s32[]{:S(2)}) async-start(), calls=%async_computation.5 | async-start | bytes 2621440 | tf_op jit(solution)/shard_map/all_gather | solution.py:229
  58.1 16.4 %copy-start.15 = (s32[8,128,16]{1,2,0:T(8,128)S(1)}, s32[8,128,16]{1,2,0:T(8,128)}, u32[]{:S(2)}) copy-start(s32[8,128,16]{1,2,0:T(8,128)} %param.12) | copy-start | bytes 196612
  107.4 181.4 %all-to-all-start.1 = ((bf16[8,8,16,2,16,128]{5,4,3,2,1,0:T(8,128)(2,1)}), bf16[8,8,16,2,16,128]{5,4,3,2,1,0:T(8,128)(2,1)}, u32[]{:S(2)}, u32[]{:S(2)}) async-start(bf16[8,8,16,2,16,128]{5,4,3,2,1,0:T(8,128)(2,1)} %bitcast.67), calls=%async_computation.1 | async-start | bytes 16777216 | tf_op jit(solution)/shard_map/all_to_all | solution.py:181
  112.7 7.9 %copy-start.16 = (bf16[2,2,128,128,1,1]{3,2,0,1,5,4:T(8,128)(2,1)S(1)}, bf16[2,2,128,128,1,1]{3,2,0,1,5,4:T(8,128)(2,1)}, u32[]{:S(2)}) copy-start(bf16[2,2,128,128,1,1]{3,2,0,1,5,4:T(8,128)(2,1)} %constant.55) | copy-start | bytes 393220
  288.8 188.4 %all-to-all-start.2 = ((bf16[8,8,16,2,16,128]{5,4,3,2,1,0:T(8,128)(2,1)}), bf16[8,8,16,2,16,128]{5,4,3,2,1,0:T(8,128)(2,1)}, u32[]{:S(2)}, u32[]{:S(2)}) async-start(bf16[8,8,16,2,16,128]{5,4,3,2,1,0:T(8,128)(2,1)} %bitcast.66), calls=%async_computation.2 | async-start | bytes 16777216 | tf_op jit(solution)/shard_map/all_to_all | solution.py:181
  293.8 309.5 %all-reduce.10.cloned.1.call-start = ((), (), s32[]{:S(2)}) async-start(), calls=%async_computation.6 | async-start | bytes 4194304 | tf_op jit(solution)/shard_map/psum | solution.py:250
  293.9 50.6 %collective-permute-start = (f32[1,2,128,128]{3,2,1,0:T(8,128)S(1)}, f32[1,2,128,128]{3,2,1,0:T(8,128)S(1)}, u32[]{:S(2)}, u32[]{:S(2)}) collective-permute-start(f32[1,2,128,128]{3,2,1,0:T(8,128)S(1)} %slice.65), channel_id=1, source_target_pairs={{1,0},{2,1},{3,2},{4,3},{5,4},{6,5},{7,6},{9,8},{10,9},{11,10},{12... | collective-permute-start | bytes 393224 | tf_op jit(solution)/shard_map/ppermute | solution.py:25
  350.1 51.0 %collective-permute-start.1 = (f32[1,2,128,128]{3,2,1,0:T(8,128)S(1)}, f32[1,2,128,128]{3,2,1,0:T(8,128)S(1)}, u32[]{:S(2)}, u32[]{:S(2)}) collective-permute-start(f32[1,2,128,128]{3,2,1,0:T(8,128)S(1)} %slice.82), channel_id=1, source_target_pairs={{0,1},{1,2},{2,3},{3,4},{4,5},{5,6},{6,7},{8,9},{9,10},{10,11},{11... | collective-permute-start | bytes 393224 | tf_op jit(solution)/shard_map/ppermute | solution.py:25
  398.8 2.3 copy-start.8
  401.1 5.5 copy-start.6
  401.1 5.5 copy-start.7
  477.1 23.9 %copy-start.5 = (f32[16,2,128,128]{3,2,1,0:T(8,128)S(1)}, f32[16,2,128,128]{3,2,1,0:T(8,128)}, u32[]{:S(2)}) copy-start(f32[16,2,128,128]{3,2,1,0:T(8,128)} %copy-done.4) | copy-start | bytes 6291460
  499.7 1.4 copy-start.2
  502.8 194.6 %reduce-scatter.2.cloned.1.call-start = ((), (), s32[]{:S(2)}) async-start(), calls=%async_computation.7 | async-start | bytes 2621440 | tf_op jit(solution)/shard_map/reduce_scatter | solution.py:257
  607.5 2.2 copy-start.10
  607.8 2.4 copy-start.13
  607.9 2.6 copy-start.9
  607.9 7.2 collective-permute-start.2
  609.7 5.3 copy-start.12
  610.5 4.6 copy-start.1
  610.5 4.6 slice-start
  623.0 34.9 %collective-permute-start.3 = (f32[1,2,128,128]{3,2,1,0:T(8,128)S(1)}, f32[1,2,128,128]{3,2,1,0:T(8,128)S(1)}, u32[]{:S(2)}, u32[]{:S(2)}) collective-permute-start(f32[1,2,128,128]{3,2,1,0:T(8,128)S(1)} %slice.92), channel_id=1, source_target_pairs={{0,1},{1,2},{2,3},{3,4},{4,5},{5,6},{6,7},{8,9},{9,10},{10,11},{11... | collective-permute-start | bytes 393224 | tf_op jit(solution)/shard_map/ppermute | solution.py:25
  627.3 30.7 %copy-start.14 = (f32[16,2,128,128]{3,2,1,0:T(8,128)S(1)}, f32[16,2,128,128]{3,2,1,0:T(8,128)}, u32[]{:S(2)}) copy-start(f32[16,2,128,128]{3,2,1,0:T(8,128)} %fusion.3) | copy-start | bytes 6291460
  657.8 1.6 copy-start.3
  (3 other events, 3.9 us)
Sparse Core Ops, SparseCore 0:
  46.2 21.5 all-gather.1
  502.9 100.3 all-reduce.9
  667.8 29.5 reduce-scatter.1
